TPU v7x, 32 devices: a whole 2x2x4 slice. The times are simulated.
32 devices in a mesh: section: 4 (over y, x), row: 8 (over z, core).
Axes of the slice: x: 2, y: 2, z: 4, core: 2. Of those that a mesh axis runs over, the one named last changes fastest.
Arguments:
- omega: bfloat16 [2048, 8192], P('section', 'row'), may hold values from -0.5 to 0.5
- basis: bfloat16 [8192, 1024], P('row', 'section'), may hold values from -6 to 6
- vectors: bfloat16 [4, 8192], P(None, 'row'), may hold values from -6 to 6
Outputs:
- ortho: float32 [4, 8192], P(None, ('row', 'section'))
- coeffs: float32 [4, 1024], P(None, 'section')
All inputs are finite; a program needn't handle non-finite values.
Results may differ from a plain program's by a relative error of at most 0.0021.
Values may be sent and summed in bfloat16 or wider, within the bound.
A program may use at most 64 MiB of HBM per device.

v0:
```python
import jax
import jax.numpy as jnp
from jax import lax
from jax.sharding import PartitionSpec as P


def from_behind(value, axis, steps):
    count = lax.axis_size(axis)
    initial, last = (max(0, -steps), min(count, count - steps))
    return lax.ppermute(value, axis, [(source, source + steps) for source in range(initial, last)])


def from_root(value, axis, source):
    kept = jnp.where(lax.axis_index(axis) == source, value, 0).astype(value.dtype)
    return lax.psum(kept, axis)


def lower_solve(factor, right):
    return lax.linalg.triangular_solve(factor, right, left_side=True, lower=True, transpose_a=False)


def factor_solve(factor, right):
    half = lower_solve(factor, right)
    return lax.linalg.triangular_solve(factor, half, left_side=True, lower=True, transpose_a=True)


def body(omega, basis, vectors):
    hi = lax.Precision.HIGHEST
    sections = lax.axis_size("section")
    my_section = lax.axis_index("section")
    whole = lax.all_gather(omega, "section", axis=0, tiled=True)
    sketch = lax.psum_scatter(
        jnp.dot(whole, basis, preferred_element_type=jnp.float32),
        "row",
        scatter_dimension=0,
        tiled=True,
    )
    probe_term = lax.dot_general(
        vectors, whole, (((1,), (1,)), ((), ())), preferred_element_type=jnp.float32
    )
    probe = lax.psum_scatter(probe_term, "row", scatter_dimension=1, tiled=True)
    gram = lax.psum(jnp.dot(sketch.T, sketch, precision=hi), "row")
    factor = jnp.linalg.cholesky(gram)

    def project(current):
        inner = jnp.dot(current, sketch, precision=hi)
        inner = lax.psum(inner, "row")
        coef = factor_solve(factor, inner.T).T
        return (coef, current - jnp.dot(coef, sketch.T, precision=hi))

    def advance(step, carry):
        current, kept = carry
        coef, moved = project(current)
        active = my_section == step
        kept = jnp.where(active, coef, kept)
        moved = jnp.where(active, moved, current)
        return (from_behind(moved, "section", 1), kept)

    start_coef = jnp.zeros((vectors.shape[0], basis.shape[1]), jnp.float32)
    probe, kept = lax.fori_loop(0, sections - 1, advance, (probe, start_coef))
    coef, moved = project(probe)
    finished = my_section == sections - 1
    kept = jnp.where(finished, coef, kept)
    final = from_root(moved, "section", sections - 1)
    rounded = kept.astype(jnp.bfloat16)
    own_term = lax.dot_general(
        rounded, basis, (((1,), (1,)), ((), ())), preferred_element_type=jnp.float32
    )
    removed = lax.psum_scatter(own_term, "section", scatter_dimension=1, tiled=True)
    width = removed.shape[1]
    mine = lax.dynamic_slice_in_dim(vectors, my_section * width, width, 1)
    remain = mine.astype(jnp.float32) - removed
    small = lax.psum(jnp.dot(final, final.T, precision=hi), "row")
    lower = jnp.linalg.cholesky(small)
    ortho = lower_solve(lower, remain)
    return (ortho, kept)


def solution(mesh):
    return jax.shard_map(
        body,
        mesh=mesh,
        in_specs=(P("section", "row"), P("row", "section"), P(None, "row")),
        out_specs=(P(None, ("row", "section")), P(None, "section")),
        check_vma=False,
    )
```

profile of v0, /device:TPU:0, one launch (start us, length us, event | category | flops | bytes accessed | tf_op | source)
XLA Modules:
  0.0 442.4 jit_solution(2750653464107480190)
XLA Ops:
  8.0 57.2 %all-gather.2.cloned.1.call-done = bf16[2048,1024]{1,0:T(8,128)(2,1)} async-done(((bf16[512,1024]{1,0:T(8,128)(2,1)}), bf16[2048,1024]{1,0:T(8,128)(2,1)}) %all-gather.2.cloned.1.call-update) | async-done | bytes 4194320 | tf_op jit(solution)/shard_map/all_gather | solution.py:31
  65.2 4.8 %fusion.36 = f32[2048,256]{1,0:T(8,128)} fusion(bf16[2048,1024]{1,0:T(8,128)(2,1)} %all-gather.2.cloned.1.call-done, bf16[1024,256]{1,0:T(8,128)(2,1)S(1)} %copy-done), kind=kOutput, calls=%fused_computation.78 | convolution fusion | flops 1073741824 | bytes 6815744 | tf_op jit(solution)/shard_map/dot_general | solution.py:33
  70.0 4.4 convolution_bitcast_fusion
  74.5 31.6 %reduce-scatter.8.cloned.1.call-done = f32[256,256]{1,0:T(8,128)} async-done(((f32[2048,256]{1,0:T(8,128)}), f32[256,256]{1,0:T(8,128)}) %reduce-scatter.8.cloned.1.call-update) | async-done | bytes 262160 | tf_op jit(solution)/shard_map/reduce_scatter | solution.py:32
  108.8 30.9 %reduce-scatter.10.cloned.1.call-done = f32[256,4]{1,0:T(8,128)} async-done(((f32[2048,4]{1,0:T(8,128)}), f32[256,4]{1,0:T(8,128)}) %reduce-scatter.10.cloned.1.call-update) | async-done | bytes 4112
  140.7 54.8 %all-reduce.3.cloned.1.call-done = f32[256,256]{0,1:T(8,128)} async-done(((f32[256,256]{0,1:T(8,128)}), f32[256,256]{0,1:T(8,128)}) %all-reduce.3.cloned.1.call-update) | async-done | bytes 262160 | tf_op jit(solution)/shard_map/psum | solution.py:42
  197.6 11.7 %cholesky.64 = f32[128,128]{1,0:T(8,128)S(1)} custom-call(f32[128,128]{1,0:T(8,128)S(1)} %cholesky.153), custom_call_target="Cholesky" | custom-call | tf_op jit(solution)/shard_map/jit(cholesky)/cholesky | solution.py:43
  209.4 9.8 %custom-call.23 = f32[1,128,128]{1,2,0:T(8,128)S(1)} custom-call(f32[1,128,128]{2,1,0:T(8,128)S(1)} %get-tuple-element.206), custom_call_target="InvertDiagBlocksLowerTriangular" | custom-call | tf_op jit(solution)/shard_map/jit(cholesky)/cholesky | solution.py:43
  219.7 11.7 %cholesky.131 = f32[128,128]{1,0:T(8,128)S(1)} custom-call(f32[128,128]{1,0:T(8,128)S(1)} %convolution_subtract_fusion.3), custom_call_target="Cholesky" | custom-call | tf_op jit(solution)/shard_map/jit(cholesky)/cholesky | solution.py:43
  233.5 4.2 while.27
  237.8 19.7 %custom-call.31 = f32[2,128,128]{1,2,0:T(8,128)S(1)} custom-call(f32[2,128,128]{2,1,0:T(8,128)S(1)} %get-tuple-element.168), custom_call_target="InvertDiagBlocksLowerTriangular" | custom-call | tf_op jit(solution)/shard_map/triangular_solve/custom-call.4 | solution.py:24
  257.4 133.4 %while.26 = (s32[]{:T(128)}, f32[4,256]{1,0:T(4,128)S(1)}, f32[4,256]{1,0:T(4,128)S(1)}, s32[]{:T(128)}, f32[256,256]{1,0:T(8,128)S(1)}, /*index=5*/f32[256,256]{1,0:T(8,128)S(1)}, s32[]{:T(128)}, s32[]{:T(128)}, s32[]{:T(128)}) while((s32[]{:T(128)}, f32[4,256]{1,0:T(4,128)S(1)}, f32[4,256]{1,0:T(4,128)S(1)}, s32[]{:T(128)}, ...), condition=%wide.region_9.12_spmd.clone, body=%wide.region_7.0_spmd.clone.sunk | while | flops 11149320 | bytes 1659231 | solution.py:60
  257.6 4.1 while.28
  261.6 19.7 %custom-call.37 = f32[2,128,128]{1,2,0:T(8,128)S(1)} custom-call(f32[2,128,128]{2,1,0:T(8,128)S(1)} %get-tuple-element.303), custom_call_target="InvertDiagBlocksLowerTriangular" | custom-call | tf_op jit(solution)/shard_map/while/body/eval_jaxpr/triangular_solve/custom-call.4 | solution.py:24
  281.5 13.7 %psum.45 = f32[256,4]{0,1:T(4,128)S(1)} all-reduce(f32[256,4]{0,1:T(4,128)S(1)} %fusion.99), channel_id=1, replica_groups=mesh['section'=4,'row'=8] {'row'}, use_global_device_ids=true, to_apply=%region_8.8 | all-reduce | flops 1024 | bytes 8192 | tf_op jit(solution)/shard_map/while/body/eval_jaxpr/psum | solution.py:47
  305.6 19.7 %custom-call.37 = f32[2,128,128]{1,2,0:T(8,128)S(1)} custom-call(f32[2,128,128]{2,1,0:T(8,128)S(1)} %get-tuple-element.303), custom_call_target="InvertDiagBlocksLowerTriangular" | custom-call | tf_op jit(solution)/shard_map/while/body/eval_jaxpr/triangular_solve/custom-call.4 | solution.py:24
  325.5 13.6 %psum.45 = f32[256,4]{0,1:T(4,128)S(1)} all-reduce(f32[256,4]{0,1:T(4,128)S(1)} %fusion.99), channel_id=1, replica_groups=mesh['section'=4,'row'=8] {'row'}, use_global_device_ids=true, to_apply=%region_8.8 | all-reduce | flops 1024 | bytes 8192 | tf_op jit(solution)/shard_map/while/body/eval_jaxpr/psum | solution.py:47
  340.6 4.2 collective-permute-start
  350.3 19.7 %custom-call.37 = f32[2,128,128]{1,2,0:T(8,128)S(1)} custom-call(f32[2,128,128]{2,1,0:T(8,128)S(1)} %get-tuple-element.303), custom_call_target="InvertDiagBlocksLowerTriangular" | custom-call | tf_op jit(solution)/shard_map/while/body/eval_jaxpr/triangular_solve/custom-call.4 | solution.py:24
  370.2 13.6 %psum.45 = f32[256,4]{0,1:T(4,128)S(1)} all-reduce(f32[256,4]{0,1:T(4,128)S(1)} %fusion.99), channel_id=1, replica_groups=mesh['section'=4,'row'=8] {'row'}, use_global_device_ids=true, to_apply=%region_8.8 | all-reduce | flops 1024 | bytes 8192 | tf_op jit(solution)/shard_map/while/body/eval_jaxpr/psum | solution.py:47
  385.2 4.3 collective-permute-start
  391.1 13.6 %psum.40 = f32[256,4]{0,1:T(4,128)S(1)} all-reduce(f32[256,4]{0,1:T(4,128)S(1)} %fusion.38), channel_id=1, replica_groups=mesh['section'=4,'row'=8] {'row'}, use_global_device_ids=true, to_apply=%region_10.13 | all-reduce | flops 1024 | bytes 8192 | tf_op jit(solution)/shard_map/psum | solution.py:47
  407.2 11.0 %psum.41 = f32[4,256]{1,0:T(4,128)S(1)} all-reduce(f32[4,256]{1,0:T(4,128)S(1)} %fusion.10), channel_id=1, replica_groups=mesh['section'=4,'row'=8] {'section'}, use_global_device_ids=true, to_apply=%region_11.14 | all-reduce | flops 1024 | bytes 8192 | tf_op jit(solution)/shard_map/psum | solution.py:15
  418.3 13.6 %psum.42 = f32[4,4]{0,1:T(4,128)S(1)} all-reduce(f32[4,4]{0,1:T(4,128)S(1)} %fusion.39), channel_id=1, replica_groups=mesh['section'=4,'row'=8] {'row'}, use_global_device_ids=true, to_apply=%region_12.15 | all-reduce | flops 16 | bytes 128 | tf_op jit(solution)/shard_map/psum | solution.py:73
  (124 shorter events, 51.5 us)
Async XLA Ops:
  7.2 58.0 %copy-start = (bf16[1024,256]{1,0:T(8,128)(2,1)S(1)}, bf16[1024,256]{1,0:T(8,128)(2,1)}, u32[]{:S(2)}) copy-start(bf16[1024,256]{1,0:T(8,128)(2,1)} %param.10) | copy-start | bytes 1572868
  7.2 58.0 %all-gather.2.cloned.1.call-start = ((), (), s32[]{:S(2)}) async-start(), calls=%async_computation.3 | async-start | bytes 5242880 | tf_op jit(solution)/shard_map/all_gather | solution.py:31
  7.9 62.1 %copy-start.3 = (bf16[4,1024]{1,0:T(4,128)(2,1)S(1)}, bf16[4,1024]{1,0:T(4,128)(2,1)}, u32[]{:S(2)}) copy-start(bf16[4,1024]{1,0:T(4,128)(2,1)} %param.11) | copy-start | bytes 24580
  7.9 98.2 %reduce-scatter.8.cloned.1.call-start = ((), (), s32[]{:S(2)}) async-start(), calls=%async_computation.4 | async-start | bytes 2359296 | tf_op jit(solution)/shard_map/reduce_scatter | solution.py:32
  70.0 69.7 %reduce-scatter.10.cloned.1.call-start = ((), (), s32[]{:S(2)}) async-start(), calls=%async_computation.6 | async-start | bytes 1179648
  74.5 121.0 %all-reduce.3.cloned.1.call-start = ((), (), s32[]{:S(2)}) async-start(), calls=%async_computation.5 | async-start | bytes 524288 | tf_op jit(solution)/shard_map/psum | solution.py:42
  106.1 151.3 %copy-start.1 = (f32[256,256]{1,0:T(8,128)S(1)}, f32[256,256]{1,0:T(8,128)}, u32[]{:S(2)}) copy-start(f32[256,256]{1,0:T(8,128)} %reduce-scatter.8.cloned.1.call-done) | copy-start | bytes 786436
  108.5 325.5 %reduce-scatter.12.cloned.1.call-start = ((), (), s32[]{:S(2)}) async-start(), calls=%async_computation.7 | async-start | bytes 655360
  296.7 4.7 %collective-permute-start = (f32[4,256]{1,0:T(4,128)S(1)}, f32[4,256]{1,0:T(4,128)S(1)}, u32[]{:S(2)}, u32[]{:S(2)}) collective-permute-start(f32[4,256]{1,0:T(4,128)S(1)} %fusion.104), channel_id=1, source_target_pairs={{0,8},{8,16},{16,24},{1,9},{9,17},{17,25},{2,10},{10,18},{18,26},{... | collective-permute-start | bytes 12296 | tf_op jit(solution)/shard_map/while/body/eval_jaxpr/ppermute | solution.py:10
  340.6 5.6 %collective-permute-start = (f32[4,256]{1,0:T(4,128)S(1)}, f32[4,256]{1,0:T(4,128)S(1)}, u32[]{:S(2)}, u32[]{:S(2)}) collective-permute-start(f32[4,256]{1,0:T(4,128)S(1)} %fusion.104), channel_id=1, source_target_pairs={{0,8},{8,16},{16,24},{1,9},{9,17},{17,25},{2,10},{10,18},{18,26},{... | collective-permute-start | bytes 12296 | tf_op jit(solution)/shard_map/while/body/eval_jaxpr/ppermute | solution.py:10
  385.2 5.6 %collective-permute-start = (f32[4,256]{1,0:T(4,128)S(1)}, f32[4,256]{1,0:T(4,128)S(1)}, u32[]{:S(2)}, u32[]{:S(2)}) collective-permute-start(f32[4,256]{1,0:T(4,128)S(1)} %fusion.104), channel_id=1, source_target_pairs={{0,8},{8,16},{16,24},{1,9},{9,17},{17,25},{2,10},{10,18},{18,26},{... | collective-permute-start | bytes 12296 | tf_op jit(solution)/shard_map/while/body/eval_jaxpr/ppermute | solution.py:10
  405.9 30.0 %copy-start.2 = (f32[4,256]{1,0:T(4,128)}, f32[4,256]{1,0:T(4,128)S(1)}, u32[]{:S(2)}) copy-start(f32[4,256]{1,0:T(4,128)S(1)} %bitcast_select_fusion.1) | copy-start | bytes 12292
Sparse Core Ops, SparseCore 0:
  9.8 55.2 all-gather.1
  70.1 35.9 reduce-scatter.7
  108.4 31.2 reduce-scatter.9
  141.9 53.5 all-reduce.2
  407.1 25.7 reduce-scatter.11
where the time goes:
time: 443 us; the launch traced here: 442 us
  waiting for transfers between devices  179 us (40%)
  other arithmetic  116 us (26%)
  blocking collectives  79.1 us (18%)
  matrix products  20.6 us (5%)
  local copies, waits for them, and re-layouts  19.6 us (4%)
  between operations  15.2 us (3%)
  starting transfers between devices  12.4 us (3%)
    another operation x16, other arithmetic, factor_solve(): lax.linalg.triangular_solve(factor, half, left_side=True, lower=True, tra...  78.8 us
    all_gather x1, waiting for transfers between devices, body(): whole = lax.all_gather(omega, 'section', axis=0, tiled=True)  57.2 us
    psum x1, waiting for transfers between devices, body(): gram = lax.psum(jnp.dot(sketch.T, sketch, precision=hi), 'row')  54.8 us
    psum x4, blocking collectives, project(): inner = lax.psum(inner, 'row')  54.5 us
    another operation x6, other arithmetic, body(): factor = jnp.linalg.cholesky(gram)  34 us
    unnamed x7, waiting for transfers between devices  31.7 us
    reduce_scatter x1, waiting for transfers between devices, body(): lax.psum_scatter(jnp.dot(whole, basis, preferred_element_type=jnp.float32...  31.6 us
    another operation x28, local copies, waits for them, and re-layouts, factor_solve(): lax.linalg.triangular_solve(factor, half, left_side=True, lower=True, tra...  16.4 us
  transfers between devices with their start and end apart: 8, of which 7 were waited for; matrix products, arithmetic and copies ran while one was open for 2% of the time, Pallas kernels for 0%

commit v1 on v0

v1 whole, which is shorter than its diff:
```python
import functools

import jax
import jax.numpy as jnp
from jax import lax
from jax.experimental import pallas as pl
from jax.experimental.pallas import tpu as pltpu
from jax.sharding import PartitionSpec as P

MESH = pl.DeviceIdType.MESH
HI = lax.Precision.HIGHEST
F32 = jnp.float32
BF16 = jnp.bfloat16
PAD = 8


def remote(src, dst, send, recv, axis, index):
    return pltpu.make_async_remote_copy(
        src_ref=src, dst_ref=dst, send_sem=send, recv_sem=recv,
        device_id={axis: index}, device_id_type=MESH,
    )


def each(first, count, fn):
    def step(t, carry):
        fn(t)
        return carry

    lax.fori_loop(first, count, step, 0)


def greet(pairs):
    barrier = pltpu.get_barrier_semaphore()
    total = 0
    for axis, count in pairs:
        me = lax.axis_index(axis)

        def hello(t, axis=axis, count=count, me=me):
            pl.semaphore_signal(
                barrier, inc=1, device_id={axis: lax.rem(me + t, count)}, device_id_type=MESH
            )

        each(1, count, hello)
        total += count - 1
    pl.semaphore_wait(barrier, total)


def sketch_kernel(
    ns, nr, omega, basis, vec, s_out, x_out, c_out, p_out, b_out,
    bg, acc, pslot, hs, zslot, xs, xsend, cs, csend, pvs, pbuf, cg,
    bsend, brecv, psend, precv, qsend, qrecv, zsend, zrecv,
    asend, arecv, fsend, frecv, xsnd, xrcv, csnd, crcv,
    gsend, grecv, hsend, hrecv, ksend, krecv,
):
    me = lax.axis_index("section")
    row = lax.axis_index("row")
    nz = nr // 2
    z, c = row // 2, lax.rem(row, 2)
    partner = z * 2 + 1 - c
    m, width = omega.shape[0], basis.shape[1]
    half = m // 2
    ch = half // nz
    span = pbuf.shape[0]
    mine = c * nz + z
    greet((("section", ns), ("row", nr)))

    def basis_copy(t):
        peer = lax.rem(me + t, ns)
        return remote(basis, bg.at[me], bsend.at[t], brecv.at[me], "section", peer)

    each(1, ns, lambda t: basis_copy(t).start())
    bg[me] = basis[...]
    pvs[row] = lax.dot_general(
        vec[...], omega[...], (((1,), (1,)), ((), ())), preferred_element_type=F32
    )[:PAD]

    def probe_copy(t, slot):
        return remote(
            pvs.at[slot], pvs.at[slot], psend.at[t], precv.at[slot], "row", lax.rem(row + t, nr)
        )

    each(1, nr, lambda t: probe_copy(t, row).start())

    def pair_copy(j):
        other = pl.multiple_of((1 - c) * half, half)
        return remote(
            acc.at[j, pl.ds(other, half)], pslot.at[j], qsend.at[j], qrecv.at[j], "row", partner
        )

    def z_copy(j, t, slot):
        to = lax.rem(z + t, nz)
        return remote(
            hs.at[j, to], zslot.at[j, slot], zsend.at[j, t], zrecv.at[j, slot], "row", to * 2 + c
        )

    def a_copy(j, t, slot):
        to = lax.rem(z + t, nz)
        chunk = s_out.at[j, c * nz + slot]
        return remote(chunk, chunk, asend.at[j, t], arecv.at[j, slot], "row", to * 2 + c)

    def f_copy(j, core, slot):
        chunk = s_out.at[j, core * nz + slot]
        return remote(chunk, chunk, fsend.at[j, slot], frecv.at[j, slot], "row", partner)

    def c_copy(t):
        to = lax.rem(me + t, ns)
        return remote(csend.at[to], cs.at[me], csnd.at[t], crcv.at[me], "section", to)

    def block(t):
        return lax.rem(me + t, ns)

    def partial_stage(t):
        j = block(t)

        @pl.when(t > 0)
        def _():
            remote(basis, bg.at[j], bsend.at[0], brecv.at[j], "section", j).wait_recv()

        acc[j] = jnp.dot(omega[...], bg[j], preferred_element_type=F32)
        pair_copy(j).start()
        pair_copy(j).wait_recv()
        own = pl.multiple_of(c * half, half)
        total = acc[j, pl.ds(own, half)] + pslot[j]
        pslot[j] = total
        hs[j] = total.reshape(nz, ch, width)
        each(1, nz, lambda s: z_copy(j, s, z).start())

    def sum_stage(t):
        j = block(t)
        each(1, nz, lambda s: z_copy(j, s, lax.rem(z + s, nz)).wait_recv())
        total = pslot[j, pl.ds(pl.multiple_of(z * ch, ch), ch)]
        for s in range(1, nz):
            total = total + zslot[j, lax.rem(z + s, nz)]
        s_out[j, mine] = total.astype(BF16)
        each(1, nz, lambda s: a_copy(j, s, z).start())
        f_copy(j, c, z).start()
        first = mine * ch
        base = pl.multiple_of(first // span * span, span)
        inner = pl.multiple_of(lax.rem(first, span), ch)
        pbuf[...] = jnp.zeros_like(pbuf)
        pbuf[pl.ds(inner, ch), :] = total
        csend[j] = jnp.dot(
            p_out[:, pl.ds(base, span)], pbuf[...], precision=HI, preferred_element_type=F32
        )
        pl.when(t > 0)(lambda: c_copy(t).start())

    def forward_stage(t):
        j = block(t)

        def one(s):
            slot = lax.rem(z + s, nz)
            a_copy(j, s, slot).wait_recv()
            f_copy(j, c, slot).start()

        each(1, nz, one)

    def loop(t):
        pl.when(t < ns)(lambda: partial_stage(t))
        pl.when((t >= 1) & (t < ns + 1))(lambda: sum_stage(t - 1))
        pl.when(t >= 2)(lambda: forward_stage(t - 2))

    partial_stage(0)
    each(1, nr, lambda t: probe_copy(t, lax.rem(row + t, nr)).wait_recv())
    probe = pvs[0]
    for k in range(1, nr):
        probe = probe + pvs[k]
    p_out[...] = probe
    each(1, ns + 2, loop)
    each(0, ns, lambda j: each(0, nz, lambda s: f_copy(j, 1 - c, s).wait_recv()))

    w = ns * width // nr
    left = row * w // width
    if w < width:
        off = pl.multiple_of(lax.rem(row * w, width), w)
        part = s_out[left, :, :, pl.ds(off, w)]
    else:
        part = s_out[left]
    part = part.reshape(m, w).astype(F32).T.astype(BF16)

    def x_copy(t):
        to = lax.rem(me + t, ns)
        return remote(xsend.at[to], xs.at[me], xsnd.at[t], xrcv.at[me], "section", to)

    def gram_of(i):
        right = s_out[i].reshape(m, width)
        xsend[i] = jnp.dot(part, right, preferred_element_type=F32)

    def gram_stage(t):
        gram_of(lax.rem(me + t, ns))
        x_copy(t).start()

    each(1, ns, gram_stage)
    gram_of(me)

    def gather(t):
        i = lax.rem(me + t, ns)
        remote(xsend.at[i], xs.at[i], xsnd.at[0], xrcv.at[i], "section", i).wait_recv()
        remote(csend.at[i], cs.at[i], csnd.at[0], crcv.at[i], "section", i).wait_recv()

    each(1, ns, gather)
    xt, ct = xsend[me], csend[me]
    for t in range(1, ns):
        i = lax.rem(me + t, ns)
        xt = xt + xs[i]
        ct = ct + cs[i]
    cg[row] = ct
    x_out[row] = xt

    def k_copy(t, slot):
        return remote(
            cg.at[slot], cg.at[slot], ksend.at[t], krecv.at[slot], "row", lax.rem(row + t, nr)
        )

    each(1, nr, lambda t: k_copy(t, row).start())

    def g_copy(t, slot):
        to = lax.rem(z + t, nz)
        piece = x_out.at[slot * 2 + c]
        return remote(piece, piece, gsend.at[t], grecv.at[slot], "row", to * 2 + c)

    def h_copy(core, slot):
        piece = x_out.at[slot * 2 + core]
        return remote(piece, piece, hsend.at[slot], hrecv.at[slot], "row", partner)

    each(1, nz, lambda s: g_copy(s, z).start())
    h_copy(c, z).start()

    rows = b_out.shape[1]
    start = pl.multiple_of(me * rows, rows)
    b_out[...] = bg[:, pl.ds(start, rows), :]

    def pass_on(s):
        slot = lax.rem(z + s, nz)
        g_copy(s, slot).wait_recv()
        h_copy(c, slot).start()

    each(1, nz, pass_on)
    each(0, nz, lambda s: h_copy(1 - c, s).wait_recv())
    each(1, nr, lambda t: k_copy(t, lax.rem(row + t, nr)).wait_recv())
    ct = cg[0]
    for k in range(1, nr):
        ct = ct + cg[k]
    c_out[...] = ct

    each(1, nr, lambda t: k_copy(t, row).wait_send())
    each(1, ns, lambda t: basis_copy(t).wait_send())
    each(1, nr, lambda t: probe_copy(t, row).wait_send())

    def drain(j):
        pair_copy(j).wait_send()
        each(1, nz, lambda s: z_copy(j, s, z).wait_send())
        each(1, nz, lambda s: a_copy(j, s, z).wait_send())
        each(0, nz, lambda s: f_copy(j, c, s).wait_send())

    each(0, ns, drain)
    each(1, ns, lambda t: x_copy(t).wait_send())
    each(1, ns, lambda t: c_copy(t).wait_send())
    each(1, nz, lambda s: g_copy(s, z).wait_send())
    each(0, nz, lambda s: h_copy(c, s).wait_send())


def solve_kernel(
    ns, n, x, inv, c0, s_in, p0, b, vec, ortho, coef,
    rbuf, cur, sm, rsend, rrecv, ssend, srecv,
):
    me = lax.axis_index("section")
    m, width = p0.shape[1], c0.shape[1]
    greet((("section", ns),))
    cur[...] = c0[...]

    def r_copy(t, slot):
        return remote(
            rbuf.at[slot], rbuf.at[slot], rsend.at[t], rrecv.at[slot],
            "section", lax.rem(me + t, ns),
        )

    def chain(j):
        @pl.when(me == j)
        def _():
            mid = lax.dot_general(
                cur[...], inv[...], (((1,), (1,)), ((), ())), precision=HI,
                preferred_element_type=F32,
            )
            rbuf[me] = jnp.dot(mid, inv[...], precision=HI, preferred_element_type=F32)
            each(1, ns, lambda t: r_copy(t, me).start())

        @pl.when(me != j)
        def _():
            remote(rbuf.at[j], rbuf.at[j], rsend.at[0], rrecv.at[j], "section", j).wait_recv()

        @pl.when(me > j)
        def _():
            cur[...] -= jnp.dot(rbuf[j], x[j], precision=HI, preferred_element_type=F32)

    each(0, ns, chain)

    def fold(j, carry):
        probe, remain = carry
        r = rbuf[j]
        sj = s_in[j].reshape(m, width).astype(F32)
        nt = (((1,), (1,)), ((), ()))
        probe = probe - lax.dot_general(r, sj, nt, precision=HI, preferred_element_type=F32)
        rb = jnp.concatenate([r, r], axis=0).astype(BF16)
        remain = remain - lax.dot_general(rb, b[j], nt, preferred_element_type=F32)[:PAD]
        return probe, remain

    probe, remain = lax.fori_loop(0, ns, fold, (p0[...], vec[...]))
    small = lax.dot_general(
        probe, probe, (((1,), (1,)), ((), ())), precision=HI, preferred_element_type=F32
    )
    sm[me] = jnp.concatenate([small, jnp.zeros((PAD, 128 - PAD), F32)], axis=1)

    def s_copy(t, slot):
        return remote(
            sm.at[slot], sm.at[slot], ssend.at[t], srecv.at[slot],
            "section", lax.rem(me + t, ns),
        )

    each(1, ns, lambda t: s_copy(t, me).start())
    coef[...] = rbuf[me, :n]
    each(1, ns, lambda t: s_copy(t, lax.rem(me + t, ns)).wait_recv())
    full = sm[0]
    for k in range(1, ns):
        full = full + sm[k]
    low = {}
    rows = []
    for i in range(n):
        for k in range(i + 1):
            value = full[i:i + 1, k:k + 1]
            for q in range(k):
                value = value - low[i, q] * low[k, q]
            low[i, k] = jnp.sqrt(value) if i == k else value / low[k, k]
        line = remain[i:i + 1]
        for k in range(i):
            line = line - low[i, k] * rows[k]
        rows.append(line / low[i, i])
        ortho[i:i + 1, :] = rows[i]
    each(1, ns, lambda t: r_copy(t, me).wait_send())
    each(1, ns, lambda t: s_copy(t, me).wait_send())


def body(ns, nr, omega, basis, vectors):
    dma = pltpu.SemaphoreType.DMA
    n, k = vectors.shape
    m, width = omega.shape[0], basis.shape[1]
    nz = nr // 2
    half = m // 2
    ch = half // nz
    w = ns * width // nr
    rows = k // ns
    vmem = pl.BlockSpec(memory_space=pltpu.VMEM)
    padded = jnp.pad(vectors, ((0, 2 * PAD - n), (0, 0)))
    s_all, x, c0, p0, b = pl.pallas_call(
        functools.partial(sketch_kernel, ns, nr),
        out_shape=(
            jax.ShapeDtypeStruct((ns, nr, ch, width), BF16),
            jax.ShapeDtypeStruct((nr, w, width), F32),
            jax.ShapeDtypeStruct((PAD, width), F32),
            jax.ShapeDtypeStruct((PAD, m), F32),
            jax.ShapeDtypeStruct((ns, rows, width), BF16),
        ),
        in_specs=[vmem] * 3,
        out_specs=(vmem,) * 5,
        scratch_shapes=[
            pltpu.VMEM((ns, k, width), BF16),
            pltpu.VMEM((ns, m, width), F32),
            pltpu.VMEM((ns, half, width), F32),
            pltpu.VMEM((ns, nz, ch, width), F32),
            pltpu.VMEM((ns, nz, ch, width), F32),
            pltpu.VMEM((ns, w, width), F32),
            pltpu.VMEM((ns, w, width), F32),
            pltpu.VMEM((ns, PAD, width), F32),
            pltpu.VMEM((ns, PAD, width), F32),
            pltpu.VMEM((nr, PAD, m), F32),
            pltpu.VMEM((max(ch, 128), width), F32),
            pltpu.VMEM((nr, PAD, width), F32),
            dma((ns,)), dma((ns,)), dma((nr,)), dma((nr,)), dma((ns,)), dma((ns,)),
            dma((ns, nz)), dma((ns, nz)), dma((ns, nz)), dma((ns, nz)),
            dma((ns, nz)), dma((ns, nz)), dma((ns,)), dma((ns,)), dma((ns,)), dma((ns,)),
            dma((nz,)), dma((nz,)), dma((nz,)), dma((nz,)), dma((nr,)), dma((nr,)),
        ],
        compiler_params=pltpu.CompilerParams(
            collective_id=0, has_side_effects=True, vmem_limit_bytes=60 * 2**20
        ),
    )(omega, basis, padded)
    x = x.reshape(ns, width, width)
    me = lax.axis_index("section")
    gram = lax.dynamic_index_in_dim(x, me, 0, keepdims=False)
    factor = jnp.linalg.cholesky(gram, symmetrize_input=False)
    inv = lax.linalg.triangular_solve(
        factor, jnp.eye(width, dtype=F32), left_side=True, lower=True, transpose_a=False
    )
    mine = lax.dynamic_slice_in_dim(vectors, me * rows, rows, 1).astype(F32)
    mine = jnp.pad(mine, ((0, PAD - n), (0, 0)))
    return pl.pallas_call(
        functools.partial(solve_kernel, ns, n),
        out_shape=(
            jax.ShapeDtypeStruct((n, rows), F32),
            jax.ShapeDtypeStruct((n, width), F32),
        ),
        in_specs=[vmem] * 7,
        out_specs=(vmem,) * 2,
        scratch_shapes=[
            pltpu.VMEM((ns, PAD, width), F32),
            pltpu.VMEM((PAD, width), F32),
            pltpu.VMEM((ns, PAD, 128), F32),
            dma((ns,)), dma((ns,)), dma((ns,)), dma((ns,)),
        ],
        compiler_params=pltpu.CompilerParams(
            collective_id=1, has_side_effects=True, vmem_limit_bytes=60 * 2**20
        ),
    )(x, inv, c0, s_all, p0, b, mine)


def solution(mesh):
    return jax.shard_map(
        functools.partial(body, mesh.shape["section"], mesh.shape["row"]),
        mesh=mesh,
        in_specs=(P("section", "row"), P("row", "section"), P(None, "row")),
        out_specs=(P(None, ("row", "section")), P(None, "section")),
        check_vma=False,
    )
```

time: 443 us -> 181 us (0.41)
  waiting for transfers between devices: 179 us -> 0 us
  Pallas kernels: 0 us -> 114 us
  blocking collectives: 79.1 us -> 0 us
  other arithmetic: 116 us -> 55.2 us
  matrix products: 20.6 us -> 1.31 us
  between operations: 15.2 us -> 2.08 us
  starting transfers between devices: 12.4 us -> 0 us
  local copies, waits for them, and re-layouts: 19.6 us -> 8.13 us
    pallas_call x0 -> x2, Pallas kernels: none -> 114 us  [the longest x1 89.5 us: body(): pl.pallas_call(functools.partial(sketch_kernel, ns, nr), out_shape=(jax.S...]
    psum x6 -> x0, blocking collectives: 79.1 us -> none  [the longest x4 54.5 us: project(): inner = lax.psum(inner, 'row')]
    another operation x27 -> x10, other arithmetic: 115 us -> 54.6 us  [the longest x6 34 us: body(): factor = jnp.linalg.cholesky(gram, symmetrize_input=False)]
    all_gather x1 -> x0, waiting for transfers between devices: 57.2 us -> none  [body(): whole = lax.all_gather(omega, 'section', axis=0, tiled=True)]
    psum x1 -> x0, waiting for transfers between devices: 54.8 us -> none  [body(): gram = lax.psum(jnp.dot(sketch.T, sketch, precision=hi), 'row')]
    unnamed x7 -> x0, waiting for transfers between devices: 31.7 us -> none
    reduce_scatter x1 -> x0, waiting for transfers between devices: 31.6 us -> none  [body(): lax.psum_scatter(jnp.dot(whole, basis, preferred_element_type=jnp.float32...]
    another operation x30 -> x9, local copies, waits for them, and re-layouts: 16.4 us -> 3.99 us  [the longest x28 16.4 us: factor_solve(): lax.linalg.triangular_solve(factor, half, left_side=True, lower=True, tra...]
  transfers between devices with their start and end apart: 8 -> 0, of which waited for: 7 -> 0; matrix products, arithmetic and copies ran while one was open for 2% -> 0% of each run, Pallas kernels for 0% -> 0%
where the time goes in v1:
time: 181 us
  Pallas kernels  114 us (63%)
  other arithmetic  55.2 us (30%)
  local copies, waits for them, and re-layouts  8.13 us (4%)
  between operations  2.08 us (1%)
    pallas_call x1, Pallas kernels, body(): pl.pallas_call(functools.partial(sketch_kernel, ns, nr), out_shape=(jax.S...  89.5 us
    another operation x6, other arithmetic, body(): factor = jnp.linalg.cholesky(gram, symmetrize_input=False)  34 us
    pallas_call x1, Pallas kernels, body(): pl.pallas_call(functools.partial(solve_kernel, ns, n), out_shape=(jax.Sha...  24.3 us
    another operation x4, other arithmetic, body(): lax.linalg.triangular_solve(factor, jnp.eye(width, dtype=F32), left_side=...  20.6 us
    another operation x6, local copies, waits for them, and re-layouts  3.9 us

profile of v1, /device:TPU:0, one launch (start us, length us, event | category | flops | bytes accessed | tf_op | source)
XLA Modules:
  0.0 180.5 jit_solution(14742000519163945092)
XLA Ops:
  0.6 0.7 copy-done
  1.3 0.6 pad.11.vec
  1.9 89.5 %shard_map.50 = (bf16[4,8,64,256]{3,2,1,0:T(8,128)(2,1)}, f32[8,128,256]{2,1,0:T(8,128)}, f32[8,256]{1,0:T(8,128)}, f32[8,512]{1,0:T(8,128)}, bf16[4,256,256]{2,1,0:T(8,128)(2,1)}) custom-call(bf16[512,1024]{1,0:T(8,128)(2,1)} %omega.1, bf16[1024,256]{1,0:T(8,128)(2,1)} %basis.1, bf16[16,1024]{1,0:T(8,128)(2,1)} %pad.11.vec), custom_call_target="tpu_custom_call" | custom-call | tf_op jit(solution)/shard_map/pallas_call | solution.py:353
  91.4 1.0 dynamic-slice_bitcast_fusion
  92.4 11.7 %cholesky.50 = f32[128,128]{1,0:T(8,128)S(1)} custom-call(f32[128,128]{1,0:T(8,128)S(1)} %cholesky.118), custom_call_target="Cholesky" | custom-call | tf_op jit(solution)/shard_map/jit(cholesky)/cholesky | solution.py:389
  104.2 9.8 %custom-call.14 = f32[1,128,128]{1,2,0:T(8,128)S(1)} custom-call(f32[1,128,128]{2,1,0:T(8,128)S(1)} %get-tuple-element.33), custom_call_target="InvertDiagBlocksLowerTriangular" | custom-call | tf_op jit(solution)/shard_map/jit(cholesky)/cholesky | solution.py:389
  114.0 0.2 constant_dynamic-update-slice_fusion
  114.2 0.3 convolution_subtract_fusion.1
  114.5 11.7 %cholesky.105 = f32[128,128]{1,0:T(8,128)S(1)} custom-call(f32[128,128]{1,0:T(8,128)S(1)} %convolution_subtract_fusion.1), custom_call_target="Cholesky" | custom-call | tf_op jit(solution)/shard_map/jit(cholesky)/cholesky | solution.py:389
  126.3 0.6 compare_reduce_fusion
  128.3 3.9 %while.1 = (s32[]{:T(128)}, f32[256,256]{1,0:T(8,128)S(1)}, s32[2,2]{1,0:T(2,128)S(1)}, f32[2,128,128]{2,1,0:T(8,128)S(1)}, s32[]{:T(128)}) while((s32[]{:T(128)}, f32[256,256]{1,0:T(8,128)S(1)}, s32[2,2]{1,0:T(2,128)S(1)}, f32[2,128,128]{2,1,0:T(8,128)S(1)}, s32[]{:T(128)}) %tuple.25), condition=%wide.while_cond, body=%wide.while_body.sunk | while | flops 2 | bytes 131181 | solution.py:390
  128.3 0.6 fusion.13
  128.9 1.4 bitcast_dynamic-update-slice_fusion.2
  130.3 0.6 fusion.13
  130.9 1.4 bitcast_dynamic-update-slice_fusion.2
  132.3 19.9 %custom-call.15 = f32[2,128,128]{1,2,0:T(8,128)S(1)} custom-call(f32[2,128,128]{2,1,0:T(8,128)S(1)} %get-tuple-element.19), custom_call_target="InvertDiagBlocksLowerTriangular" | custom-call | tf_op jit(solution)/shard_map/triangular_solve | solution.py:390
  152.2 0.3 fusion
  152.4 0.3 convolution_subtract_fusion
  152.7 0.3 fusion.3
  153.0 0.7 pad_maximum_fusion.inv
  153.7 0.6 pad_convert_fusion.vec
  154.3 24.3 %shard_map.51 = (f32[4,256]{1,0:T(4,128)}, f32[4,256]{1,0:T(4,128)}) custom-call(f32[4,256,256]{2,1,0:T(8,128)} %bitcast.31, f32[256,256]{1,0:T(8,128)} %pad_maximum_fusion.inv, f32[8,256]{1,0:T(8,128)} %get-tuple-element.8.c0, bf16[4,8,64,256]{3,2,1,0:T(8,128)(2,1)} %get-tuple-element.9.s_in, f32[8,512]{1,0:T(8,128)} %get-tuple-element.10.p0, ...), custom_call_target="tpu_custom_call" | custom-call | tf_op jit(solution)/shard_map/pallas_call | solution.py:395
  178.7 1.3 copy.17
  179.9 0.6 copy.18
  (15 shorter events, 0.3 us)
Async XLA Ops:
  0.6 0.7 copy-start
  178.7 1.3 copy-start.1

commit v2 on v1

--- a/solution.py
+++ b/solution.py
@@ -259,6 +259,55 @@
     each(0, nz, lambda s: h_copy(c, s).wait_send())
 
 
+def invert_tile(mat):
+    size = mat.shape[0]
+    lane = lax.broadcasted_iota(jnp.int32, (size, size), 1)
+    sub = lax.broadcasted_iota(jnp.int32, (PAD, size), 0)
+    short = lax.broadcasted_iota(jnp.int32, (PAD, size), 1)
+    for k in range(0, size, PAD):
+        cols = [jnp.broadcast_to(mat[:, k + q:k + q + 1], (size, size)) for q in range(PAD)]
+        heads = [col[k:k + PAD] for col in cols]
+        rows = jnp.where((short >= k) & (short < k + PAD), 0.0, mat[k:k + PAD])
+        rows = rows + jnp.where(short == sub + k, 1.0, 0.0)
+        for p in range(PAD):
+            scale = 1.0 / heads[p][p:p + 1]
+            line = rows[p:p + 1] * scale
+            rows = jnp.where(sub == p, line, rows - heads[p] * line)
+            for q in range(p + 1, PAD):
+                head = heads[q][p:p + 1] * scale
+                heads[q] = jnp.where(sub == p, head, heads[q] - heads[p] * head)
+        mat = jnp.where((lane >= k) & (lane < k + PAD), 0.0, mat)
+        for q in range(PAD):
+            mat = mat - cols[q] * rows[q:q + 1]
+        parts = [mat[:k], rows, mat[k + PAD:]]
+        mat = jnp.concatenate([part for part in parts if part.shape[0]], axis=0)
+    return mat
+
+
+def invert_kernel(x, inv):
+    width = inv.shape[0]
+    size = min(width, 128)
+    inv[...] = x[lax.axis_index("section")]
+    column = lax.broadcasted_iota(jnp.int32, (width, width), 1) // size
+    eye = (
+        lax.broadcasted_iota(jnp.int32, (size, size), 0)
+        == lax.broadcasted_iota(jnp.int32, (size, size), 1)
+    ).astype(F32)
+
+    def step(b, carry):
+        at = pl.ds(pl.multiple_of(b * size, size), size)
+        pivot = invert_tile(inv[at, at])
+        left = inv[:, at]
+        inv[at, at] = eye
+        rows = jnp.dot(pivot, inv[at, :], precision=HI, preferred_element_type=F32)
+        rest = jnp.where(column == b, 0.0, inv[...])
+        inv[...] = rest - jnp.dot(left, rows, precision=HI, preferred_element_type=F32)
+        inv[at, :] = rows
+        return carry
+
+    lax.fori_loop(0, width // size, step, 0)
+
+
 def solve_kernel(
     ns, n, x, inv, c0, s_in, p0, b, vec, ortho, coef,
     rbuf, cur, sm, rsend, rrecv, ssend, srecv,
@@ -277,11 +326,7 @@
     def chain(j):
         @pl.when(me == j)
         def _():
-            mid = lax.dot_general(
-                cur[...], inv[...], (((1,), (1,)), ((), ())), precision=HI,
-                preferred_element_type=F32,
-            )
-            rbuf[me] = jnp.dot(mid, inv[...], precision=HI, preferred_element_type=F32)
+            rbuf[me] = jnp.dot(cur[...], inv[...], precision=HI, preferred_element_type=F32)
             each(1, ns, lambda t: r_copy(t, me).start())
 
         @pl.when(me != j)
@@ -385,11 +430,13 @@
     )(omega, basis, padded)
     x = x.reshape(ns, width, width)
     me = lax.axis_index("section")
-    gram = lax.dynamic_index_in_dim(x, me, 0, keepdims=False)
-    factor = jnp.linalg.cholesky(gram, symmetrize_input=False)
-    inv = lax.linalg.triangular_solve(
-        factor, jnp.eye(width, dtype=F32), left_side=True, lower=True, transpose_a=False
-    )
+    inv = pl.pallas_call(
+        invert_kernel,
+        out_shape=jax.ShapeDtypeStruct((width, width), F32),
+        in_specs=[vmem],
+        out_specs=vmem,
+        compiler_params=pltpu.CompilerParams(vmem_limit_bytes=32 * 2**20),
+    )(x)
     mine = lax.dynamic_slice_in_dim(vectors, me * rows, rows, 1).astype(F32)
     mine = jnp.pad(mine, ((0, PAD - n), (0, 0)))
     return pl.pallas_call(

time: 181 us -> 129 us (0.71)
  other arithmetic: 55.2 us -> 0.6 us
  Pallas kernels: 114 us -> 122 us
  local copies, waits for them, and re-layouts: 8.13 us -> 5.09 us
    another operation x10 -> x0, other arithmetic: 54.6 us -> none  [the longest x6 34 us: body(): factor = jnp.linalg.cholesky(gram, symmetrize_input=False)]
    pallas_call x0 -> x1, Pallas kernels: none -> 10.2 us  [body(): pl.pallas_call(invert_kernel, out_shape=jax.ShapeDtypeStruct((width, widt...]
    another operation x9 -> x0, local copies, waits for them, and re-layouts: 3.99 us -> none
    pallas_call x1, Pallas kernels: 24.3 us -> 22.2 us  [body(): pl.pallas_call(functools.partial(solve_kernel, ns, n), out_shape=(jax.Sha...]
    unnamed x6 -> x10, local copies, waits for them, and re-layouts: 2.55 us -> 4.47 us
where the time goes in v2:
time: 129 us; the launch traced here: 128 us
  Pallas kernels  122 us (95%)
  local copies, waits for them, and re-layouts  5.09 us (4%)
    pallas_call x1, Pallas kernels, body(): pl.pallas_call(functools.partial(sketch_kernel, ns, nr), out_shape=(jax.S...  89.5 us
    pallas_call x1, Pallas kernels, body(): pl.pallas_call(functools.partial(solve_kernel, ns, n), out_shape=(jax.Sha...  22.2 us
    pallas_call x1, Pallas kernels, body(): pl.pallas_call(invert_kernel, out_shape=jax.ShapeDtypeStruct((width, widt...  10.2 us
    unnamed x10, local copies, waits for them, and re-layouts  4.47 us

profile of v2, /device:TPU:0, one launch (start us, length us, event | category | flops | bytes accessed | tf_op | source)
XLA Modules:
  0.0 128.3 jit_solution(1424530451380013276)
XLA Ops:
  0.6 0.0 copy-start.2
  0.6 0.7 copy-done.2
  1.3 0.6 pad_convert_fusion.vec
  1.9 0.6 pad.10.vec
  2.5 89.5 %shard_map.50 = (bf16[4,8,64,256]{3,2,1,0:T(8,128)(2,1)}, f32[8,128,256]{2,1,0:T(8,128)}, f32[8,256]{1,0:T(8,128)}, f32[8,512]{1,0:T(8,128)}, bf16[4,256,256]{2,1,0:T(8,128)(2,1)}) custom-call(bf16[512,1024]{1,0:T(8,128)(2,1)} %omega.1, bf16[1024,256]{1,0:T(8,128)(2,1)} %basis.1, bf16[16,1024]{1,0:T(8,128)(2,1)} %pad.10.vec), custom_call_target="tpu_custom_call" | custom-call | tf_op jit(solution)/shard_map/pallas_call | solution.py:398
  92.1 0.0 copy-start
  92.1 1.2 copy-done
  93.3 10.2 %shard_map.51.inv = f32[256,256]{1,0:T(8,128)S(1)} custom-call(f32[4,256,256]{2,1,0:T(8,128)S(1)} %bitcast.2), custom_call_target="tpu_custom_call" | custom-call | tf_op jit(solution)/shard_map/pallas_call | solution.py:433
  103.5 0.0 copy-start.1
  103.5 0.7 copy-done.1
  104.2 22.2 %shard_map.52 = (f32[4,256]{1,0:T(4,128)}, f32[4,256]{1,0:T(4,128)}) custom-call(f32[4,256,256]{2,1,0:T(8,128)} %bitcast.1, f32[256,256]{1,0:T(8,128)} %copy-done.1, f32[8,256]{1,0:T(8,128)} %get-tuple-element.8.c0, bf16[4,8,64,256]{3,2,1,0:T(8,128)(2,1)} %get-tuple-element.9.s_in, f32[8,512]{1,0:T(8,128)} %get-tuple-element.10.p0, ...), custom_call_target="tpu_custom_call" | custom-call | tf_op jit(solution)/shard_map/pallas_call | solution.py:442
  126.4 0.0 copy-start.3
  126.5 1.3 copy.7
  127.7 0.0 copy-done.3
  127.7 0.6 copy.8
  (1 shorter events, 0.0 us)
Async XLA Ops:
  0.6 0.7 copy-start.2
  92.1 1.2 copy-start
  103.5 0.7 copy-start.1
  126.4 1.3 %copy-start.3 = (f32[4,256]{1,0:T(4,128)S(1)}, f32[4,256]{1,0:T(4,128)}, u32[]{:S(2)}) copy-start(f32[4,256]{1,0:T(4,128)} %get-tuple-element.15) | copy-start | bytes 12292

commit v3 on v2

--- a/solution.py
+++ b/solution.py
@@ -45,12 +45,66 @@
     pl.semaphore_wait(barrier, total)
 
 
+class Line:
+    def __init__(self, z, nz, c, chunk, up, down, recv, fsend, frecv):
+        self.z, self.nz, self.c, self.chunk = z, nz, c, chunk
+        self.up, self.down, self.recv = up, down, recv
+        self.fsend, self.frecv = fsend, frecv
+
+    def rise(self, slot):
+        piece = self.chunk(self.c, slot)
+        to = (self.z + 1) * 2 + self.c
+        return remote(piece, piece, self.up(slot), self.recv(slot), "row", to)
+
+    def sink(self, slot):
+        piece = self.chunk(self.c, slot)
+        to = (self.z - 1) * 2 + self.c
+        return remote(piece, piece, self.down(slot), self.recv(slot), "row", to)
+
+    def across(self, core, slot):
+        piece = self.chunk(core, slot)
+        to = self.z * 2 + 1 - self.c
+        return remote(piece, piece, self.fsend(slot), self.frecv(slot), "row", to)
+
+    def send(self, slot, upward, downward):
+        if upward:
+            pl.when(self.z < self.nz - 1)(lambda: self.rise(slot).start())
+        if downward:
+            pl.when(self.z > 0)(lambda: self.sink(slot).start())
+        self.across(self.c, slot).start()
+
+    def begin(self):
+        self.send(self.z, True, True)
+
+    def relay(self, s):
+        @pl.when(self.z >= s)
+        def _():
+            self.sink(self.z - s).wait_recv()
+            self.send(self.z - s, True, False)
+
+        @pl.when(self.z + s < self.nz)
+        def _():
+            self.sink(self.z + s).wait_recv()
+            self.send(self.z + s, False, True)
+
+    def finish(self):
+        each(0, self.nz, lambda q: self.across(1 - self.c, q).wait_recv())
+
+    def drain(self):
+        def one(q):
+            pl.when((q <= self.z) & (self.z < self.nz - 1))(lambda: self.rise(q).wait_send())
+            pl.when((q >= self.z) & (self.z > 0))(lambda: self.sink(q).wait_send())
+            self.across(self.c, q).wait_send()
+
+        each(0, self.nz, one)
+
+
 def sketch_kernel(
     ns, nr, omega, basis, vec, s_out, x_out, c_out, p_out, b_out,
     bg, acc, pslot, hs, zslot, xs, xsend, cs, csend, pvs, pbuf, cg,
-    bsend, brecv, psend, precv, qsend, qrecv, zsend, zrecv,
-    asend, arecv, fsend, frecv, xsnd, xrcv, csnd, crcv,
-    gsend, grecv, hsend, hrecv, ksend, krecv,
+    rsend, rrecv, lsend, lrecv, psend, precv, qsend, qrecv, zsend, zrecv,
+    aup, adown, arecv, fsend, frecv, xsnd, xrcv, csnd, crcv,
+    gup, gdown, grecv, hsend, hrecv, ksend, krecv, lbsem,
 ):
     me = lax.axis_index("section")
     row = lax.axis_index("row")
@@ -64,12 +118,34 @@
     mine = c * nz + z
     greet((("section", ns), ("row", nr)))
 
-    def basis_copy(t):
-        peer = lax.rem(me + t, ns)
-        return remote(basis, bg.at[me], bsend.at[t], brecv.at[me], "section", peer)
-
-    each(1, ns, lambda t: basis_copy(t).start())
-    bg[me] = basis[...]
+    far = ns // 2
+    tall = basis.shape[0] // 2
+
+    def at_place(p):
+        return jnp.where(p < far, p, ns + far - 1 - p)
+
+    place = at_place(me)
+
+    def near(d):
+        return at_place(lax.rem(place + d + ns, ns))
+
+    def right_copy(d, part):
+        origin = near(-d)
+        block = bg.at[origin, pl.ds(0, tall)] if part else bg.at[origin]
+        return remote(block, block, rsend.at[d], rrecv.at[origin], "section", near(1))
+
+    def left_copy(d, part):
+        origin = near(d)
+        block = bg.at[origin, pl.ds(tall, tall)] if part else bg.at[origin]
+        return remote(block, block, lsend.at[d], lrecv.at[origin], "section", near(-1))
+
+    def first_copy(send, recv, to):
+        return remote(basis, bg.at[me], send.at[0], recv.at[me], "section", to)
+
+    first_copy(rsend, rrecv, near(1)).start()
+    first_copy(lsend, lrecv, near(-1)).start()
+    own_block = pltpu.make_async_copy(basis, bg.at[me], lbsem)
+    own_block.start()
     pvs[row] = lax.dot_general(
         vec[...], omega[...], (((1,), (1,)), ((), ())), preferred_element_type=F32
     )[:PAD]
@@ -93,31 +169,49 @@
             hs.at[j, to], zslot.at[j, slot], zsend.at[j, t], zrecv.at[j, slot], "row", to * 2 + c
         )
 
-    def a_copy(j, t, slot):
-        to = lax.rem(z + t, nz)
-        chunk = s_out.at[j, c * nz + slot]
-        return remote(chunk, chunk, asend.at[j, t], arecv.at[j, slot], "row", to * 2 + c)
-
-    def f_copy(j, core, slot):
-        chunk = s_out.at[j, core * nz + slot]
-        return remote(chunk, chunk, fsend.at[j, slot], frecv.at[j, slot], "row", partner)
-
-    def c_copy(t):
-        to = lax.rem(me + t, ns)
-        return remote(csend.at[to], cs.at[me], csnd.at[t], crcv.at[me], "section", to)
+    def line(j):
+        return Line(
+            z, nz, c, lambda core, slot: s_out.at[j, core * nz + slot],
+            lambda q: aup.at[j, q], lambda q: adown.at[j, q], lambda q: arecv.at[j, q],
+            lambda q: fsend.at[j, q], lambda q: frecv.at[j, q],
+        )
+
+    def c_copy(j):
+        return remote(csend.at[j], cs.at[me], csnd.at[j], crcv.at[me], "section", j)
 
     def block(t):
-        return lax.rem(me + t, ns)
+        d = (t + 1) // 2
+        return near(jnp.where(lax.rem(t, 2) == 1, ns - d, d))
+
+    def arrive(d):
+        @pl.when(d < far)
+        def _():
+            right_copy(d, False).wait_recv()
+            left_copy(d, False).wait_recv()
+
+            @pl.when(d + 1 < far)
+            def _():
+                right_copy(d, False).start()
+                left_copy(d, False).start()
+
+            @pl.when(d + 1 == far)
+            def _():
+                right_copy(d, True).start()
+                left_copy(d, True).start()
+
+        @pl.when(d == far)
+        def _():
+            right_copy(far, True).wait_recv()
+            left_copy(far, True).wait_recv()
 
     def partial_stage(t):
         j = block(t)
-
-        @pl.when(t > 0)
-        def _():
-            remote(basis, bg.at[j], bsend.at[0], brecv.at[j], "section", j).wait_recv()
-
+        pl.when(lax.rem(t, 2) == 1)(lambda: arrive((t + 1) // 2))
         acc[j] = jnp.dot(omega[...], bg[j], preferred_element_type=F32)
         pair_copy(j).start()
+
+    def pair_stage(t):
+        j = block(t)
         pair_copy(j).wait_recv()
         own = pl.multiple_of(c * half, half)
         total = acc[j, pl.ds(own, half)] + pslot[j]
@@ -132,8 +226,7 @@
         for s in range(1, nz):
             total = total + zslot[j, lax.rem(z + s, nz)]
         s_out[j, mine] = total.astype(BF16)
-        each(1, nz, lambda s: a_copy(j, s, z).start())
-        f_copy(j, c, z).start()
+        line(j).begin()
         first = mine * ch
         base = pl.multiple_of(first // span * span, span)
         inner = pl.multiple_of(lax.rem(first, span), ch)
@@ -142,31 +235,26 @@
         csend[j] = jnp.dot(
             p_out[:, pl.ds(base, span)], pbuf[...], precision=HI, preferred_element_type=F32
         )
-        pl.when(t > 0)(lambda: c_copy(t).start())
-
-    def forward_stage(t):
-        j = block(t)
-
-        def one(s):
-            slot = lax.rem(z + s, nz)
-            a_copy(j, s, slot).wait_recv()
-            f_copy(j, c, slot).start()
-
-        each(1, nz, one)
+        pl.when(t > 0)(lambda: c_copy(j).start())
 
     def loop(t):
+        for s in range(1, nz):
+            b = t - 1 - s
+            pl.when((b >= 0) & (b < ns))(lambda b=b, s=s: line(block(b)).relay(s))
         pl.when(t < ns)(lambda: partial_stage(t))
         pl.when((t >= 1) & (t < ns + 1))(lambda: sum_stage(t - 1))
-        pl.when(t >= 2)(lambda: forward_stage(t - 2))
-
+        pl.when(t < ns)(lambda: pair_stage(t))
+
+    own_block.wait()
     partial_stage(0)
+    pair_stage(0)
     each(1, nr, lambda t: probe_copy(t, lax.rem(row + t, nr)).wait_recv())
     probe = pvs[0]
     for k in range(1, nr):
         probe = probe + pvs[k]
     p_out[...] = probe
-    each(1, ns + 2, loop)
-    each(0, ns, lambda j: each(0, nz, lambda s: f_copy(j, 1 - c, s).wait_recv()))
+    each(1, ns + nz, loop)
+    each(0, ns, lambda j: line(j).finish())
 
     w = ns * width // nr
     left = row * w // width
@@ -195,7 +283,7 @@
     def gather(t):
         i = lax.rem(me + t, ns)
         remote(xsend.at[i], xs.at[i], xsnd.at[0], xrcv.at[i], "section", i).wait_recv()
-        remote(csend.at[i], cs.at[i], csnd.at[0], crcv.at[i], "section", i).wait_recv()
+        remote(csend.at[i], cs.at[i], csnd.at[i], crcv.at[i], "section", i).wait_recv()
 
     each(1, ns, gather)
     xt, ct = xsend[me], csend[me]
@@ -213,29 +301,19 @@
 
     each(1, nr, lambda t: k_copy(t, row).start())
 
-    def g_copy(t, slot):
-        to = lax.rem(z + t, nz)
-        piece = x_out.at[slot * 2 + c]
-        return remote(piece, piece, gsend.at[t], grecv.at[slot], "row", to * 2 + c)
-
-    def h_copy(core, slot):
-        piece = x_out.at[slot * 2 + core]
-        return remote(piece, piece, hsend.at[slot], hrecv.at[slot], "row", partner)
-
-    each(1, nz, lambda s: g_copy(s, z).start())
-    h_copy(c, z).start()
+    final = Line(
+        z, nz, c, lambda core, slot: x_out.at[slot * 2 + core],
+        lambda q: gup.at[q], lambda q: gdown.at[q], lambda q: grecv.at[q],
+        lambda q: hsend.at[q], lambda q: hrecv.at[q],
+    )
+    final.begin()
 
     rows = b_out.shape[1]
     start = pl.multiple_of(me * rows, rows)
     b_out[...] = bg[:, pl.ds(start, rows), :]
 
-    def pass_on(s):
-        slot = lax.rem(z + s, nz)
-        g_copy(s, slot).wait_recv()
-        h_copy(c, slot).start()
-
-    each(1, nz, pass_on)
-    each(0, nz, lambda s: h_copy(1 - c, s).wait_recv())
+    each(1, nz, final.relay)
+    final.finish()
     each(1, nr, lambda t: k_copy(t, lax.rem(row + t, nr)).wait_recv())
     ct = cg[0]
     for k in range(1, nr):
@@ -243,20 +321,22 @@
     c_out[...] = ct
 
     each(1, nr, lambda t: k_copy(t, row).wait_send())
-    each(1, ns, lambda t: basis_copy(t).wait_send())
+    first_copy(rsend, rrecv, near(1)).wait_send()
+    first_copy(lsend, lrecv, near(-1)).wait_send()
+    for d in range(1, far):
+        right_copy(d, d + 1 == far).wait_send()
+        left_copy(d, d + 1 == far).wait_send()
     each(1, nr, lambda t: probe_copy(t, row).wait_send())
 
     def drain(j):
         pair_copy(j).wait_send()
         each(1, nz, lambda s: z_copy(j, s, z).wait_send())
-        each(1, nz, lambda s: a_copy(j, s, z).wait_send())
-        each(0, nz, lambda s: f_copy(j, c, s).wait_send())
+        line(j).drain()
 
     each(0, ns, drain)
     each(1, ns, lambda t: x_copy(t).wait_send())
-    each(1, ns, lambda t: c_copy(t).wait_send())
-    each(1, nz, lambda s: g_copy(s, z).wait_send())
-    each(0, nz, lambda s: h_copy(c, s).wait_send())
+    each(1, ns, lambda t: c_copy(block(t)).wait_send())
+    final.drain()
 
 
 def invert_tile(mat):
@@ -419,10 +499,12 @@
             pltpu.VMEM((nr, PAD, m), F32),
             pltpu.VMEM((max(ch, 128), width), F32),
             pltpu.VMEM((nr, PAD, width), F32),
-            dma((ns,)), dma((ns,)), dma((nr,)), dma((nr,)), dma((ns,)), dma((ns,)),
-            dma((ns, nz)), dma((ns, nz)), dma((ns, nz)), dma((ns, nz)),
-            dma((ns, nz)), dma((ns, nz)), dma((ns,)), dma((ns,)), dma((ns,)), dma((ns,)),
-            dma((nz,)), dma((nz,)), dma((nz,)), dma((nz,)), dma((nr,)), dma((nr,)),
+            dma((ns,)), dma((ns,)), dma((ns,)), dma((ns,)), dma((nr,)), dma((nr,)),
+            dma((ns,)), dma((ns,)), dma((ns, nz)), dma((ns, nz)),
+            dma((ns, nz)), dma((ns, nz)), dma((ns, nz)), dma((ns, nz)), dma((ns, nz)),
+            dma((ns,)), dma((ns,)), dma((ns,)), dma((ns,)),
+            dma((nz,)), dma((nz,)), dma((nz,)), dma((nz,)), dma((nz,)), dma((nr,)), dma((nr,)),
+            dma,
         ],
         compiler_params=pltpu.CompilerParams(
             collective_id=0, has_side_effects=True, vmem_limit_bytes=60 * 2**20

time: 129 us -> 120 us (0.930)
  Pallas kernels: 122 us -> 113 us
    pallas_call x1, Pallas kernels: 89.5 us -> 80.3 us  [body(): pl.pallas_call(functools.partial(sketch_kernel, ns, nr), out_shape=(jax.S...]
where the time goes in v3:
time: 120 us
  Pallas kernels  113 us (94%)
  local copies, waits for them, and re-layouts  5.09 us (4%)
    pallas_call x1, Pallas kernels, body(): pl.pallas_call(functools.partial(sketch_kernel, ns, nr), out_shape=(jax.S...  80.3 us
    pallas_call x1, Pallas kernels, body(): pl.pallas_call(functools.partial(solve_kernel, ns, n), out_shape=(jax.Sha...  23 us
    pallas_call x1, Pallas kernels, body(): pl.pallas_call(invert_kernel, out_shape=jax.ShapeDtypeStruct((width, widt...  10.2 us
    unnamed x10, local copies, waits for them, and re-layouts  4.47 us

profile of v3, /device:TPU:0, one launch (start us, length us, event | category | flops | bytes accessed | tf_op | source)
XLA Modules:
  0.0 119.8 jit_solution(13304810295845047278)
XLA Ops:
  0.6 0.0 copy-start.2
  0.6 0.7 copy-done.2
  1.3 0.6 pad_convert_fusion.vec
  1.9 0.6 pad.10.vec
  2.5 80.3 %shard_map.50 = (bf16[4,8,64,256]{3,2,1,0:T(8,128)(2,1)}, f32[8,128,256]{2,1,0:T(8,128)}, f32[8,256]{1,0:T(8,128)}, f32[8,512]{1,0:T(8,128)}, bf16[4,256,256]{2,1,0:T(8,128)(2,1)}) custom-call(bf16[512,1024]{1,0:T(8,128)(2,1)} %omega.1, bf16[1024,256]{1,0:T(8,128)(2,1)} %basis.1, bf16[16,1024]{1,0:T(8,128)(2,1)} %pad.10.vec), custom_call_target="tpu_custom_call" | custom-call | tf_op jit(solution)/shard_map/pallas_call | solution.py:478
  82.8 0.0 copy-start
  82.8 1.2 %copy-done = f32[8,128,256]{2,1,0:T(8,128)S(1)} copy-done((f32[8,128,256]{2,1,0:T(8,128)S(1)}, f32[8,128,256]{2,1,0:T(8,128)}, u32[]{:S(2)}) %copy-start) | copy-done | bytes 1048600
  84.0 10.2 %shard_map.51.inv = f32[256,256]{1,0:T(8,128)S(1)} custom-call(f32[4,256,256]{2,1,0:T(8,128)S(1)} %bitcast.2), custom_call_target="tpu_custom_call" | custom-call | tf_op jit(solution)/shard_map/pallas_call | solution.py:515
  94.3 0.0 copy-start.1
  94.3 0.7 copy-done.1
  95.0 23.0 %shard_map.52 = (f32[4,256]{1,0:T(4,128)}, f32[4,256]{1,0:T(4,128)}) custom-call(f32[4,256,256]{2,1,0:T(8,128)} %bitcast.1, f32[256,256]{1,0:T(8,128)} %copy-done.1, f32[8,256]{1,0:T(8,128)} %get-tuple-element.8.c0, bf16[4,8,64,256]{3,2,1,0:T(8,128)(2,1)} %get-tuple-element.9.s_in, f32[8,512]{1,0:T(8,128)} %get-tuple-element.10.p0, ...), custom_call_target="tpu_custom_call" | custom-call | tf_op jit(solution)/shard_map/pallas_call | solution.py:524
  117.9 0.0 copy-start.3
  117.9 1.3 %copy.7 = f32[4,256]{1,0:T(4,128)} copy(f32[4,256]{1,0:T(4,128)} %get-tuple-element.14) | data formatting | bytes 8192
  119.2 0.0 copy-done.3
  119.2 0.6 copy.8
  (1 shorter events, 0.0 us)
Async XLA Ops:
  0.6 0.7 copy-start.2
  82.8 1.2 %copy-start = (f32[8,128,256]{2,1,0:T(8,128)S(1)}, f32[8,128,256]{2,1,0:T(8,128)}, u32[]{:S(2)}) copy-start(f32[8,128,256]{2,1,0:T(8,128)} %get-tuple-element.7) | copy-start | bytes 3145732
  94.3 0.7 copy-start.1
  117.9 1.3 %copy-start.3 = (f32[4,256]{1,0:T(4,128)S(1)}, f32[4,256]{1,0:T(4,128)}, u32[]{:S(2)}) copy-start(f32[4,256]{1,0:T(4,128)} %get-tuple-element.15) | copy-start | bytes 12292

commit v4 on v3

--- a/solution.py
+++ b/solution.py
@@ -301,19 +301,23 @@
 
     each(1, nr, lambda t: k_copy(t, row).start())
 
-    final = Line(
-        z, nz, c, lambda core, slot: x_out.at[slot * 2 + core],
-        lambda q: gup.at[q], lambda q: gdown.at[q], lambda q: grecv.at[q],
-        lambda q: hsend.at[q], lambda q: hrecv.at[q],
-    )
-    final.begin()
+    deep = w // 2
+
+    def final(h):
+        return Line(
+            z, nz, c, lambda core, slot: x_out.at[slot * 2 + core, pl.ds(h * deep, deep)],
+            lambda q: gup.at[h, q], lambda q: gdown.at[h, q], lambda q: grecv.at[h, q],
+            lambda q: hsend.at[h, q], lambda q: hrecv.at[h, q],
+        )
+
+    each(0, 2, lambda h: final(h).begin())
 
     rows = b_out.shape[1]
     start = pl.multiple_of(me * rows, rows)
     b_out[...] = bg[:, pl.ds(start, rows), :]
 
-    each(1, nz, final.relay)
-    final.finish()
+    each(1, nz, lambda s: each(0, 2, lambda h: final(h).relay(s)))
+    each(0, 2, lambda h: final(h).finish())
     each(1, nr, lambda t: k_copy(t, lax.rem(row + t, nr)).wait_recv())
     ct = cg[0]
     for k in range(1, nr):
@@ -336,7 +340,7 @@
     each(0, ns, drain)
     each(1, ns, lambda t: x_copy(t).wait_send())
     each(1, ns, lambda t: c_copy(block(t)).wait_send())
-    final.drain()
+    each(0, 2, lambda h: final(h).drain())
 
 
 def invert_tile(mat):
@@ -390,7 +394,7 @@
 
 def solve_kernel(
     ns, n, x, inv, c0, s_in, p0, b, vec, ortho, coef,
-    rbuf, cur, sm, rsend, rrecv, ssend, srecv,
+    rbuf, cur, probe_ref, remain_ref, sm, rsend, rrecv, ssend, srecv,
 ):
     me = lax.axis_index("section")
     m, width = p0.shape[1], c0.shape[1]
@@ -403,12 +407,31 @@
             "section", lax.rem(me + t, ns),
         )
 
+    nt = (((1,), (1,)), ((), ()))
+    probe_ref[...] = p0[...]
+    remain_ref[...] = vec[...]
+
+    def fold(j):
+        r = rbuf[j]
+        high = r.astype(BF16).astype(F32)
+        mid = (r - high).astype(BF16).astype(F32)
+        low = r - high - mid
+        parts = jnp.concatenate([high, mid, low, jnp.zeros_like(r)], axis=0).astype(BF16)
+        moved = lax.dot_general(
+            parts, s_in[j].reshape(m, width), nt, preferred_element_type=F32
+        )
+        probe_ref[...] -= moved[:PAD] + (moved[PAD:2 * PAD] + moved[2 * PAD:3 * PAD])
+        taken = lax.dot_general(parts[:2 * PAD], b[j], nt, preferred_element_type=F32)
+        remain_ref[...] -= taken[:PAD]
+
     def chain(j):
         @pl.when(me == j)
         def _():
             rbuf[me] = jnp.dot(cur[...], inv[...], precision=HI, preferred_element_type=F32)
             each(1, ns, lambda t: r_copy(t, me).start())
 
+        pl.when(j > 0)(lambda: fold(j - 1))
+
         @pl.when(me != j)
         def _():
             remote(rbuf.at[j], rbuf.at[j], rsend.at[0], rrecv.at[j], "section", j).wait_recv()
@@ -418,18 +441,8 @@
             cur[...] -= jnp.dot(rbuf[j], x[j], precision=HI, preferred_element_type=F32)
 
     each(0, ns, chain)
-
-    def fold(j, carry):
-        probe, remain = carry
-        r = rbuf[j]
-        sj = s_in[j].reshape(m, width).astype(F32)
-        nt = (((1,), (1,)), ((), ()))
-        probe = probe - lax.dot_general(r, sj, nt, precision=HI, preferred_element_type=F32)
-        rb = jnp.concatenate([r, r], axis=0).astype(BF16)
-        remain = remain - lax.dot_general(rb, b[j], nt, preferred_element_type=F32)[:PAD]
-        return probe, remain
-
-    probe, remain = lax.fori_loop(0, ns, fold, (p0[...], vec[...]))
+    fold(ns - 1)
+    probe, remain = probe_ref[...], remain_ref[...]
     small = lax.dot_general(
         probe, probe, (((1,), (1,)), ((), ())), precision=HI, preferred_element_type=F32
     )
@@ -503,7 +516,8 @@
             dma((ns,)), dma((ns,)), dma((ns, nz)), dma((ns, nz)),
             dma((ns, nz)), dma((ns, nz)), dma((ns, nz)), dma((ns, nz)), dma((ns, nz)),
             dma((ns,)), dma((ns,)), dma((ns,)), dma((ns,)),
-            dma((nz,)), dma((nz,)), dma((nz,)), dma((nz,)), dma((nz,)), dma((nr,)), dma((nr,)),
+            dma((2, nz)), dma((2, nz)), dma((2, nz)), dma((2, nz)), dma((2, nz)),
+            dma((nr,)), dma((nr,)),
             dma,
         ],
         compiler_params=pltpu.CompilerParams(
@@ -532,6 +546,8 @@
         scratch_shapes=[
             pltpu.VMEM((ns, PAD, width), F32),
             pltpu.VMEM((PAD, width), F32),
+            pltpu.VMEM((PAD, m), F32),
+            pltpu.VMEM((PAD, rows), F32),
             pltpu.VMEM((ns, PAD, 128), F32),
             dma((ns,)), dma((ns,)), dma((ns,)), dma((ns,)),
         ],

time: 120 us -> 116 us (0.967)
  Pallas kernels: 113 us -> 110 us
    pallas_call x1, Pallas kernels: 23 us -> 20.1 us  [body(): pl.pallas_call(functools.partial(solve_kernel, ns, n), out_shape=(jax.Sha...]
where the time goes in v4:
time: 116 us
  Pallas kernels  110 us (95%)
  local copies, waits for them, and re-layouts  5.09 us (4%)
    pallas_call x1, Pallas kernels, body(): pl.pallas_call(functools.partial(sketch_kernel, ns, nr), out_shape=(jax.S...  79.2 us
    pallas_call x1, Pallas kernels, body(): pl.pallas_call(functools.partial(solve_kernel, ns, n), out_shape=(jax.Sha...  20.1 us
    pallas_call x1, Pallas kernels, body(): pl.pallas_call(invert_kernel, out_shape=jax.ShapeDtypeStruct((width, widt...  10.2 us
    unnamed x10, local copies, waits for them, and re-layouts  4.47 us

profile of v4, /device:TPU:0, one launch (start us, length us, event | category | flops | bytes accessed | tf_op | source)
XLA Modules:
  0.0 115.9 jit_solution(15472877341198090479)
XLA Ops:
  0.6 0.0 copy-start.2
  0.6 0.7 copy-done.2
  1.3 0.6 pad_convert_fusion.vec
  1.9 0.6 pad.10.vec
  2.5 79.2 %shard_map.50 = (bf16[4,8,64,256]{3,2,1,0:T(8,128)(2,1)}, f32[8,128,256]{2,1,0:T(8,128)}, f32[8,256]{1,0:T(8,128)}, f32[8,512]{1,0:T(8,128)}, bf16[4,256,256]{2,1,0:T(8,128)(2,1)}) custom-call(bf16[512,1024]{1,0:T(8,128)(2,1)} %omega.1, bf16[1024,256]{1,0:T(8,128)(2,1)} %basis.1, bf16[16,1024]{1,0:T(8,128)(2,1)} %pad.10.vec), custom_call_target="tpu_custom_call" | custom-call | tf_op jit(solution)/shard_map/pallas_call | solution.py:491
  81.8 0.0 copy-start
  81.8 1.2 %copy-done = f32[8,128,256]{2,1,0:T(8,128)S(1)} copy-done((f32[8,128,256]{2,1,0:T(8,128)S(1)}, f32[8,128,256]{2,1,0:T(8,128)}, u32[]{:S(2)}) %copy-start) | copy-done | bytes 1048600
  83.0 10.2 %shard_map.51.inv = f32[256,256]{1,0:T(8,128)S(1)} custom-call(f32[4,256,256]{2,1,0:T(8,128)S(1)} %bitcast.2), custom_call_target="tpu_custom_call" | custom-call | tf_op jit(solution)/shard_map/pallas_call | solution.py:529
  93.3 0.0 copy-start.1
  93.3 0.7 copy-done.1
  94.0 20.1 %shard_map.52 = (f32[4,256]{1,0:T(4,128)}, f32[4,256]{1,0:T(4,128)}) custom-call(f32[4,256,256]{2,1,0:T(8,128)} %bitcast.1, f32[256,256]{1,0:T(8,128)} %copy-done.1, f32[8,256]{1,0:T(8,128)} %get-tuple-element.8.c0, bf16[4,8,64,256]{3,2,1,0:T(8,128)(2,1)} %get-tuple-element.9.s_in, f32[8,512]{1,0:T(8,128)} %get-tuple-element.10.p0, ...), custom_call_target="tpu_custom_call" | custom-call | tf_op jit(solution)/shard_map/pallas_call | solution.py:538
  114.0 0.0 copy-start.3
  114.0 1.3 %copy.7 = f32[4,256]{1,0:T(4,128)} copy(f32[4,256]{1,0:T(4,128)} %get-tuple-element.14) | data formatting | bytes 8192
  115.3 0.0 copy-done.3
  115.3 0.6 copy.8
  (1 shorter events, 0.0 us)
Async XLA Ops:
  0.6 0.7 copy-start.2
  81.8 1.2 %copy-start = (f32[8,128,256]{2,1,0:T(8,128)S(1)}, f32[8,128,256]{2,1,0:T(8,128)}, u32[]{:S(2)}) copy-start(f32[8,128,256]{2,1,0:T(8,128)} %get-tuple-element.7) | copy-start | bytes 3145732
  93.3 0.7 copy-start.1
  114.0 1.3 %copy-start.3 = (f32[4,256]{1,0:T(4,128)S(1)}, f32[4,256]{1,0:T(4,128)}, u32[]{:S(2)}) copy-start(f32[4,256]{1,0:T(4,128)} %get-tuple-element.15) | copy-start | bytes 12292

commit v5 on v4

--- a/solution.py
+++ b/solution.py
@@ -100,7 +100,7 @@
 
 
 def sketch_kernel(
-    ns, nr, omega, basis, vec, s_out, x_out, c_out, p_out, b_out,
+    ns, nr, omega, basis, vec, s_out, x_out, c_out, p_out, b_out, g_out,
     bg, acc, pslot, hs, zslot, xs, xsend, cs, csend, pvs, pbuf, cg,
     rsend, rrecv, lsend, lrecv, psend, precv, qsend, qrecv, zsend, zrecv,
     aup, adown, arecv, fsend, frecv, xsnd, xrcv, csnd, crcv,
@@ -318,6 +318,8 @@
 
     each(1, nz, lambda s: each(0, 2, lambda h: final(h).relay(s)))
     each(0, 2, lambda h: final(h).finish())
+    per = width // w
+    g_out[...] = x_out[pl.ds(me * per, per)].reshape(width, width)
     each(1, nr, lambda t: k_copy(t, lax.rem(row + t, nr)).wait_recv())
     ct = cg[0]
     for k in range(1, nr):
@@ -371,7 +373,7 @@
 def invert_kernel(x, inv):
     width = inv.shape[0]
     size = min(width, 128)
-    inv[...] = x[lax.axis_index("section")]
+    inv[...] = x[...]
     column = lax.broadcasted_iota(jnp.int32, (width, width), 1) // size
     eye = (
         lax.broadcasted_iota(jnp.int32, (size, size), 0)
@@ -488,7 +490,7 @@
     rows = k // ns
     vmem = pl.BlockSpec(memory_space=pltpu.VMEM)
     padded = jnp.pad(vectors, ((0, 2 * PAD - n), (0, 0)))
-    s_all, x, c0, p0, b = pl.pallas_call(
+    s_all, x, c0, p0, b, g = pl.pallas_call(
         functools.partial(sketch_kernel, ns, nr),
         out_shape=(
             jax.ShapeDtypeStruct((ns, nr, ch, width), BF16),
@@ -496,9 +498,10 @@
             jax.ShapeDtypeStruct((PAD, width), F32),
             jax.ShapeDtypeStruct((PAD, m), F32),
             jax.ShapeDtypeStruct((ns, rows, width), BF16),
+            jax.ShapeDtypeStruct((width, width), F32),
         ),
         in_specs=[vmem] * 3,
-        out_specs=(vmem,) * 5,
+        out_specs=(vmem,) * 6,
         scratch_shapes=[
             pltpu.VMEM((ns, k, width), BF16),
             pltpu.VMEM((ns, m, width), F32),
@@ -532,7 +535,7 @@
         in_specs=[vmem],
         out_specs=vmem,
         compiler_params=pltpu.CompilerParams(vmem_limit_bytes=32 * 2**20),
-    )(x)
+    )(g)
     mine = lax.dynamic_slice_in_dim(vectors, me * rows, rows, 1).astype(F32)
     mine = jnp.pad(mine, ((0, PAD - n), (0, 0)))
     return pl.pallas_call(

time: 116 us -> 117 us (level)
    unnamed x10 -> x8, local copies, waits for them, and re-layouts: 4.47 us -> 3.5 us
where the time goes in v5:
time: 117 us; the launch traced here: 116 us
  Pallas kernels  110 us (94%)
  local copies, waits for them, and re-layouts  5.49 us (5%)
    pallas_call x1, Pallas kernels, body(): pl.pallas_call(functools.partial(sketch_kernel, ns, nr), out_shape=(jax.S...  79.3 us
    pallas_call x1, Pallas kernels, body(): pl.pallas_call(functools.partial(solve_kernel, ns, n), out_shape=(jax.Sha...  20.1 us
    pallas_call x1, Pallas kernels, body(): pl.pallas_call(invert_kernel, out_shape=jax.ShapeDtypeStruct((width, widt...  10.2 us
    unnamed x8, local copies, waits for them, and re-layouts  3.5 us

profile of v5, /device:TPU:0, one launch (start us, length us, event | category | flops | bytes accessed | tf_op | source)
XLA Modules:
  0.0 116.4 jit_solution(847569081550754751)
XLA Ops:
  0.6 1.3 %pad.10.vec = bf16[16,1024]{1,0:T(8,128)(2,1)} pad(bf16[4,1024]{1,0:T(4,128)(2,1)} %param.5, bf16[]{:T(256)} %constant.10.clone.1), padding=0_12x0_0 | pad | bytes 40962 | tf_op jit(solution)/shard_map/jit(_pad)/pad | solution.py:492
  1.9 79.3 %shard_map.50 = (bf16[4,8,64,256]{3,2,1,0:T(8,128)(2,1)}, f32[8,128,256]{2,1,0:T(8,128)}, f32[8,256]{1,0:T(8,128)}, f32[8,512]{1,0:T(8,128)}, bf16[4,256,256]{2,1,0:T(8,128)(2,1)}, /*index=5*/f32[256,256]{1,0:T(8,128)}) custom-call(bf16[512,1024]{1,0:T(8,128)(2,1)} %omega.1, bf16[1024,256]{1,0:T(8,128)(2,1)} %basis.1, bf16[16,1024]{1,0:T(8,128)(2,1)} %pad.10.vec), custom_call_target="tpu_custom_call" | custom-call | tf_op jit(solution)/shard_map/pallas_call | solution.py:493
  81.3 0.0 copy-start.1
  81.3 0.9 copy-done.1
  82.2 10.2 %shard_map.51.inv = f32[256,256]{1,0:T(8,128)S(1)} custom-call(f32[256,256]{1,0:T(8,128)S(1)} %copy-done.1), custom_call_target="tpu_custom_call" | custom-call | tf_op jit(solution)/shard_map/pallas_call | solution.py:532
  92.5 0.0 copy-start
  92.5 0.7 copy-done
  93.2 0.7 constant_dynamic-slice_fusion
  93.8 0.6 pad_convert_fusion.vec
  94.4 20.1 %shard_map.52 = (f32[4,256]{1,0:T(4,128)}, f32[4,256]{1,0:T(4,128)}) custom-call(f32[4,256,256]{2,1,0:T(8,128)} %bitcast.1, f32[256,256]{1,0:T(8,128)} %copy-done, f32[8,256]{1,0:T(8,128)} %get-tuple-element.10.c0, bf16[4,8,64,256]{3,2,1,0:T(8,128)(2,1)} %get-tuple-element.11.s_in, f32[8,512]{1,0:T(8,128)} %get-tuple-element.12.p0, ...), custom_call_target="tpu_custom_call" | custom-call | tf_op jit(solution)/shard_map/pallas_call | solution.py:541
  114.5 0.0 copy-start.2
  114.5 1.3 %copy.7 = f32[4,256]{1,0:T(4,128)} copy(f32[4,256]{1,0:T(4,128)} %get-tuple-element.16) | data formatting | bytes 8192
  115.8 0.0 copy-done.2
  115.8 0.6 copy.8
Async XLA Ops:
  81.3 1.0 copy-start.1
  92.5 0.7 copy-start
  114.5 1.3 %copy-start.2 = (f32[4,256]{1,0:T(4,128)S(1)}, f32[4,256]{1,0:T(4,128)}, u32[]{:S(2)}) copy-start(f32[4,256]{1,0:T(4,128)} %get-tuple-element.17) | copy-start | bytes 12292
